TPU v7x, 512 devices: a whole 4x8x8 slice. The times are simulated.
512 devices in a mesh: gx: 64 (over z_hi, y, core), gy: 8 (over z_lo, x).
Axes of the slice: x: 4, y: 8, z: 8 (z_hi: 4, z_lo: 2; z = z_hi * 2 + z_lo), core: 2. Of those that a mesh axis runs over, the one named last changes fastest.
Arguments:
- field: bfloat16 [1, 512, 512, 128], P(None, 'gx', 'gy'), may hold values from -6 to 6
- conv_weight: bfloat16 [3, 3, 128, 128], replicated, may hold values from -0.1875 to 0.1875
- qkv_weight: bfloat16 [128, 384], replicated, may hold values from -4 to 4
- out_weight: bfloat16 [128, 128], replicated, may hold values from -0.5 to 0.5
Outputs:
- result: bfloat16 [1, 512, 512, 128], P(None, 'gx', 'gy')
All inputs are finite; a program needn't handle non-finite values.
Results may differ from a plain program's by a relative error of at most 0.0064.
Values may be sent and summed in bfloat16 or wider, within the bound.
No kernel may reach another device: no remote copies, remote signals or barrier semaphores. Data moves between devices by JAX's collectives and lax.ppermute only.
A program may use at most 64 MiB of HBM per device.

v0:
```python
import jax
import jax.numpy as jnp
from jax import lax
from jax.sharding import PartitionSpec as P

HEADS = 4
HEAD = 32


def to_lines(block):
    return lax.all_to_all(block, "gx", split_axis=2, concat_axis=1, tiled=True)


def to_blocks(lines):
    return lax.all_to_all(lines, "gx", split_axis=1, concat_axis=2, tiled=True)


def neighbour_lines(line):
    n_gx, n_gy = (lax.axis_size("gx"), lax.axis_size("gy"))
    count = n_gx * n_gy

    def device(c):
        c = c % count
        return c % n_gx * n_gy + c // n_gx

    from_left = lax.ppermute(line, ("gx", "gy"), [(device(c), device(c + 1)) for c in range(count)])
    from_right = lax.ppermute(
        line, ("gx", "gy"), [(device(c + 1), device(c)) for c in range(count)]
    )
    return (from_left, from_right)


def convolve(columns, conv_weight):
    length, width = (columns.shape[1], columns.shape[2])
    taps = []
    for a in range(3):
        for b in range(3):
            taps.append(jnp.roll(columns[b], 1 - a, axis=0))
    stacked = jnp.concatenate(taps, axis=1)
    return jnp.dot(
        stacked, conv_weight.reshape(9 * width, width), preferred_element_type=jnp.float32
    )


def normalize(stem):
    mean = jnp.mean(stem, axis=-1, keepdims=True)
    varia = jnp.mean((stem - mean) ** 2, axis=-1, keepdims=True)
    return ((stem - mean) / jnp.sqrt(varia + 1e-05)).astype(jnp.bfloat16)


def attend(normed, qkv_weight):
    length, width = normed.shape
    qkv = jnp.dot(normed, qkv_weight, preferred_element_type=jnp.float32).astype(jnp.bfloat16)
    query = qkv[:, :width].reshape(length, HEADS, HEAD)
    keyed = qkv[:, width : 2 * width].reshape(length, HEADS, HEAD)
    valued = qkv[:, 2 * width :].reshape(length, HEADS, HEAD)
    scores = jnp.einsum("qhd,khd->hqk", query, keyed, preferred_element_type=jnp.float32)
    scores = scores / jnp.sqrt(jnp.float32(HEAD))
    top = jnp.max(scores, axis=-1, keepdims=True)
    expo = jnp.exp(scores - top)
    probs = (expo / jnp.sum(expo, axis=-1, keepdims=True)).astype(jnp.bfloat16)
    mixed = jnp.einsum("hqk,khd->qhd", probs, valued, preferred_element_type=jnp.float32)
    return mixed.astype(jnp.bfloat16).reshape(length, width)


def on_device(field, conv_weight, qkv_weight, out_weight):
    lines = to_lines(field)
    planes, length, _, width = lines.shape
    line = lines.reshape(length, width)
    from_left, from_right = neighbour_lines(line)
    stem = convolve(jnp.stack([from_left, line, from_right]), conv_weight)
    normed = normalize(stem)
    attended = attend(normed, qkv_weight)
    projected = jnp.dot(attended, out_weight, preferred_element_type=jnp.float32)
    result = (stem + projected).astype(jnp.bfloat16)
    return to_blocks(result.reshape(planes, length, 1, width))


def solution(mesh):
    placed = (P(None, "gx", "gy", None), P(), P(), P())
    return jax.shard_map(
        on_device, mesh=mesh, in_specs=placed, out_specs=P(None, "gx", "gy", None), check_vma=False
    )
```

profile of v0, /device:TPU:7, one launch (start us, length us, event | category | flops | bytes accessed | tf_op | source)
XLA Modules:
  0.0 78.3 jit_solution(10470661683168732793)
XLA Ops:
  0.0 0.0 copy-start
  0.0 1.0 %copy.13 = bf16[1,8,64,128]{3,1,0,2:T(8,128)(2,1)S(1)} copy(bf16[1,8,64,128]{3,2,1,0:T(8,128)(2,1)} %param.4) | data formatting | bytes 262144 | tf_op args[0]
  1.0 29.4 %all_to_all.33 = bf16[1,8,64,128]{3,1,0,2:T(8,128)(2,1)S(1)} all-to-all(bf16[1,8,64,128]{3,1,0,2:T(8,128)(2,1)S(1)} %copy.13), channel_id=1, replica_groups=mesh['gx'=64,'gy'=8] {'gx'}, dimensions={2} | all-to-all | bytes 262144 | tf_op jit(solution)/shard_map/all_to_all | solution.py:11
  30.4 3.2 %collective-permute-start = (bf16[512,128]{1,0:T(8,128)(2,1)S(1)}, bf16[512,128]{1,0:T(8,128)(2,1)S(1)}, u32[]{:S(2)}, u32[]{:S(2)}) collective-permute-start(bf16[512,128]{1,0:T(8,128)(2,1)S(1)} %bitcast.35), channel_id=1, source_target_pairs={{0,8},{8,16},{16,24},{24,32},{32,40},{40,48},{48,56},{56,64},{64,7... | collective-permute-start | bytes 393224 | tf_op jit(solution)/shard_map/ppermute | solution.py:26
  33.7 1.9 %collective-permute-start.1 = (bf16[512,128]{1,0:T(8,128)(2,1)S(1)}, bf16[512,128]{1,0:T(8,128)(2,1)S(1)}, u32[]{:S(2)}, u32[]{:S(2)}) collective-permute-start(bf16[512,128]{1,0:T(8,128)(2,1)S(1)} %bitcast.37), channel_id=1, source_target_pairs={{8,0},{16,8},{24,16},{32,24},{40,32},{48,40},{56,48},{64,56},{72,6... | collective-permute-start | bytes 393224 | tf_op jit(solution)/shard_map/ppermute | solution.py:27
  35.6 0.0 collective-permute-done
  35.7 0.1 maximum_dynamic-update-slice_fusion.4
  35.8 4.4 %collective-permute-done.1 = bf16[512,128]{1,0:T(8,128)(2,1)S(1)} collective-permute-done((bf16[512,128]{1,0:T(8,128)(2,1)S(1)}, bf16[512,128]{1,0:T(8,128)(2,1)S(1)}, u32[]{:S(2)}, u32[]{:S(2)}) %collective-permute-start.1) | collective-permute-done | bytes 131104 | tf_op jit(solution)/shard_map/ppermute | solution.py:27
  40.3 0.1 maximum_dynamic-update-slice_fusion.3
  40.6 0.0 copy-start.2
  40.6 0.0 copy-done
  40.6 0.5 fusion.21
  41.2 0.1 multiply_reduce_fusion.1
  41.3 0.2 copy-done.2
  41.5 0.3 convolution_convert_fusion
  41.8 3.4 %fusion.22 = (f32[4,512]{1,0:T(4,128)S(1)}, f32[4,512,512]{1,2,0:T(8,128)}) fusion(bf16[512,4,32]{0,2,1:T(8,128)(2,1)S(1)} %bitcast.45, bf16[512,4,32]{0,2,1:T(8,128)(2,1)S(1)} %bitcast.44), kind=kOutput, calls=%fused_computation.38 | convolution fusion | flops 70255104 | bytes 4464640 | tf_op jit(solution)/shard_map/sub | solution.py:60
  45.3 0.0 copy-start.1
  45.3 2.7 %fusion.7 = bf16[4,32,512]{2,1,0:T(8,128)(2,1)S(1)} fusion(bf16[512,4,32]{0,2,1:T(8,128)(2,1)S(1)} %bitcast.43, f32[4,512,512]{1,2,0:T(8,128)} %get-tuple-element.23, f32[4,512]{1,0:T(4,128)S(1)} %get-tuple-element.22), kind=kOutput, calls=%fused_computation.10 | convolution fusion | flops 69271552 | bytes 4464640 | tf_op jit(solution)/shard_map/hqk,khd->qhd/dot_general | solution.py:62
  47.9 0.0 copy-done.1
  47.9 0.2 fusion.8
  48.2 0.2 copy.16
  48.3 0.5 broadcast.26
  48.9 1.4 %reduce = bf16[512,128]{1,0:T(8,128)(2,1)S(1)} reduce(bf16[512,1,1,128]{3,2,1,0:T(2,128)(2,1)S(1)} %bitcast.39, bf16[]{:T(256)} %broadcast.26), dimensions={1,2}, to_apply=%bitcast.21.reduce_sub_computation | reduce | bytes 262146
  50.3 0.1 reshape.43
  50.3 27.2 %all_to_all.34 = bf16[64,2,512]{2,1,0:T(2,128)(2,1)S(1)} all-to-all(bf16[64,2,512]{2,1,0:T(2,128)(2,1)S(1)} %reshape.43), channel_id=1, replica_groups=mesh['gx'=64,'gy'=8] {'gx'}, dimensions={0} | all-to-all | bytes 262144 | tf_op jit(solution)/shard_map/all_to_all | solution.py:15
  77.5 0.1 reshape.44
  77.7 0.7 copy.17
  (17 shorter events, 0.5 us)
Async XLA Ops:
  0.0 40.6 %copy-start = (bf16[3,3,128,128]{3,2,1,0:T(8,128)(2,1)S(1)}, bf16[3,3,128,128]{3,2,1,0:T(8,128)(2,1)}, u32[]{:S(2)}) copy-start(bf16[3,3,128,128]{3,2,1,0:T(8,128)(2,1)} %param.5) | copy-start | bytes 884740
  30.4 5.2 %collective-permute-start = (bf16[512,128]{1,0:T(8,128)(2,1)S(1)}, bf16[512,128]{1,0:T(8,128)(2,1)S(1)}, u32[]{:S(2)}, u32[]{:S(2)}) collective-permute-start(bf16[512,128]{1,0:T(8,128)(2,1)S(1)} %bitcast.35), channel_id=1, source_target_pairs={{0,8},{8,16},{16,24},{24,32},{32,40},{40,48},{48,56},{56,64},{64,7... | collective-permute-start | bytes 393224 | tf_op jit(solution)/shard_map/ppermute | solution.py:26
  33.7 6.6 %collective-permute-start.1 = (bf16[512,128]{1,0:T(8,128)(2,1)S(1)}, bf16[512,128]{1,0:T(8,128)(2,1)S(1)}, u32[]{:S(2)}, u32[]{:S(2)}) collective-permute-start(bf16[512,128]{1,0:T(8,128)(2,1)S(1)} %bitcast.37), channel_id=1, source_target_pairs={{8,0},{16,8},{24,16},{32,24},{40,32},{48,40},{56,48},{64,56},{72,6... | collective-permute-start | bytes 393224 | tf_op jit(solution)/shard_map/ppermute | solution.py:27
  40.6 0.9 %copy-start.2 = (bf16[128,384]{1,0:T(8,128)(2,1)S(1)}, bf16[128,384]{1,0:T(8,128)(2,1)}, u32[]{:S(2)}) copy-start(bf16[128,384]{1,0:T(8,128)(2,1)} %param.6) | copy-start | bytes 294916
  45.3 2.7 %copy-start.1 = (bf16[128,128]{1,0:T(8,128)(2,1)S(1)}, bf16[128,128]{1,0:T(8,128)(2,1)}, u32[]{:S(2)}) copy-start(bf16[128,128]{1,0:T(8,128)(2,1)} %param.7) | copy-start | bytes 98308
where the time goes:
time: 78.6 us; the launch traced here: 78.3 us
  blocking collectives  56.6 us (72%)
  matrix products  7.16 us (9%)
  starting transfers between devices  5.12 us (7%)
  waiting for transfers between devices  4.45 us (6%)
  local copies, waits for them, and re-layouts  3.09 us (4%)
  other arithmetic  1.74 us (2%)
    all_to_all x1, blocking collectives, to_lines(): return lax.all_to_all(block, 'gx', split_axis=2, concat_axis=1, tiled=True)  29.4 us
    all_to_all x1, blocking collectives, to_blocks(): return lax.all_to_all(lines, 'gx', split_axis=1, concat_axis=2, tiled=True)  27.2 us
    ppermute x1, waiting for transfers between devices, neighbour_lines(): lax.ppermute(line, ('gx', 'gy'), [(device(c + 1), device(c)) for c in ran...  4.45 us
    sub x1, matrix products, attend(): expo = jnp.exp(scores - top)  3.43 us
    ppermute x1, starting transfers between devices, neighbour_lines(): lax.ppermute(line, ('gx', 'gy'), [(device(c), device(c + 1)) for c in ran...  3.2 us
    dot_general x1, matrix products, attend(): jnp.einsum('hqk,khd->qhd', probs, valued, preferred_element_type=jnp.floa...  2.66 us
    unnamed x14, local copies, waits for them, and re-layouts  2.06 us
    ppermute x1, starting transfers between devices, neighbour_lines(): lax.ppermute(line, ('gx', 'gy'), [(device(c + 1), device(c)) for c in ran...  1.92 us
  transfers between devices with their start and end apart: 2, of which 1 were waited for; matrix products, arithmetic and copies ran while one was open for 0% of the time, Pallas kernels for 0%

commit v1 on v0

--- a/solution.py
+++ b/solution.py
@@ -12,7 +12,9 @@
 
 
 def to_blocks(lines):
-    return lax.all_to_all(lines, "gx", split_axis=1, concat_axis=2, tiled=True)
+    return jnp.concatenate(
+        lax.all_to_all(jnp.stack(jnp.split(lines, lax.axis_size("gx"), axis=1)), "gx", 0, 0), axis=2
+    )
 
 
 def neighbour_lines(line):

time: 78.6 us -> 74.5 us (0.948); the launches traced: 78.3 us -> 73.4 us
  waiting for transfers between devices: 4.45 us -> 1.86 us
  blocking collectives: 56.6 us -> 55.2 us
  other arithmetic: 1.74 us -> 0.52 us
    ppermute x1, waiting for transfers between devices: 4.45 us -> 0.01 us  [neighbour_lines(): lax.ppermute(line, ('gx', 'gy'), [(device(c + 1), device(c)) for c in ran...]
    ppermute x1, waiting for transfers between devices: 0.01 us -> 1.86 us  [neighbour_lines(): lax.ppermute(line, ('gx', 'gy'), [(device(c), device(c + 1)) for c in ran...]
    unnamed x6 -> x5, other arithmetic: 1.64 us -> 0.23 us
    all_to_all x1, blocking collectives: 27.2 us -> 25.8 us  [to_blocks(): lax.all_to_all(jnp.stack(jnp.split(lines, lax.axis_size('gx'), axis=1)),...]
    unnamed x14 -> x73, local copies, waits for them, and re-layouts: 2.06 us -> 1.72 us
where the time goes in v1:
time: 74.5 us; the launch traced here: 73.4 us
  blocking collectives  55.2 us (74%)
  matrix products  7.34 us (10%)
  starting transfers between devices  5.55 us (7%)
  local copies, waits for them, and re-layouts  2.59 us (3%)
  waiting for transfers between devices  1.86 us (2%)
    all_to_all x1, blocking collectives, to_lines(): return lax.all_to_all(block, 'gx', split_axis=2, concat_axis=1, tiled=True)  29.4 us
    all_to_all x1, blocking collectives, to_blocks(): lax.all_to_all(jnp.stack(jnp.split(lines, lax.axis_size('gx'), axis=1)),...  25.8 us
    sub x1, matrix products, attend(): expo = jnp.exp(scores - top)  3.44 us
    ppermute x1, starting transfers between devices, neighbour_lines(): lax.ppermute(line, ('gx', 'gy'), [(device(c), device(c + 1)) for c in ran...  3.26 us
    dot_general x1, matrix products, attend(): jnp.einsum('hqk,khd->qhd', probs, valued, preferred_element_type=jnp.floa...  2.66 us
    ppermute x1, starting transfers between devices, neighbour_lines(): lax.ppermute(line, ('gx', 'gy'), [(device(c + 1), device(c)) for c in ran...  2.29 us
    ppermute x1, waiting for transfers between devices, neighbour_lines(): lax.ppermute(line, ('gx', 'gy'), [(device(c), device(c + 1)) for c in ran...  1.86 us
    unnamed x73, local copies, waits for them, and re-layouts  1.72 us
  transfers between devices with their start and end apart: 2, of which 1 were waited for; matrix products, arithmetic and copies ran while one was open for 0% of the time, Pallas kernels for 0%

profile of v1, /device:TPU:7, one launch (start us, length us, event | category | flops | bytes accessed | tf_op | source)
XLA Modules:
  0.0 73.4 jit_solution(11796493341647624815)
XLA Ops:
  0.0 0.0 copy-start
  0.0 1.0 %copy.10 = bf16[1,8,64,128]{3,1,0,2:T(8,128)(2,1)S(1)} copy(bf16[1,8,64,128]{3,2,1,0:T(8,128)(2,1)} %param.4) | data formatting | bytes 262144 | tf_op args[0]
  1.0 29.4 %all_to_all.20 = bf16[1,8,64,128]{3,1,0,2:T(8,128)(2,1)S(1)} all-to-all(bf16[1,8,64,128]{3,1,0,2:T(8,128)(2,1)S(1)} %copy.10), channel_id=1, replica_groups=mesh['gx'=64,'gy'=8] {'gx'}, dimensions={2} | all-to-all | bytes 262144 | tf_op jit(solution)/shard_map/all_to_all | solution.py:11
  30.4 2.3 %collective-permute-start.1 = (bf16[512,128]{1,0:T(8,128)(2,1)S(1)}, bf16[512,128]{1,0:T(8,128)(2,1)S(1)}, u32[]{:S(2)}, u32[]{:S(2)}) collective-permute-start(bf16[512,128]{1,0:T(8,128)(2,1)S(1)} %bitcast.285), channel_id=1, source_target_pairs={{8,0},{16,8},{24,16},{32,24},{40,32},{48,40},{56,48},{64,56},{72,6... | collective-permute-start | bytes 393224 | tf_op jit(solution)/shard_map/ppermute | solution.py:29
  32.7 3.3 %collective-permute-start = (bf16[512,128]{1,0:T(8,128)(2,1)S(1)}, bf16[512,128]{1,0:T(8,128)(2,1)S(1)}, u32[]{:S(2)}, u32[]{:S(2)}) collective-permute-start(bf16[512,128]{1,0:T(8,128)(2,1)S(1)} %bitcast.286), channel_id=1, source_target_pairs={{0,8},{8,16},{16,24},{24,32},{32,40},{40,48},{48,56},{56,64},{64,7... | collective-permute-start | bytes 393224 | tf_op jit(solution)/shard_map/ppermute | solution.py:28
  36.0 1.9 %collective-permute-done = bf16[512,128]{1,0:T(8,128)(2,1)S(1)} collective-permute-done((bf16[512,128]{1,0:T(8,128)(2,1)S(1)}, bf16[512,128]{1,0:T(8,128)(2,1)S(1)}, u32[]{:S(2)}, u32[]{:S(2)}) %collective-permute-start) | collective-permute-done | bytes 131104 | tf_op jit(solution)/shard_map/ppermute | solution.py:28
  38.0 0.1 constant_dynamic-update-slice_fusion.7
  38.1 0.0 collective-permute-done.1
  38.1 0.1 constant_dynamic-update-slice_fusion.6
  38.4 0.0 copy-start.2
  38.5 0.0 copy-done
  38.5 0.6 fusion.21
  39.1 0.2 multiply_reduce_fusion.1
  39.3 0.0 copy-done.2
  39.3 0.5 convolution_convert_fusion
  39.8 3.4 %fusion.22 = (f32[4,512]{1,0:T(4,128)S(1)}, f32[4,512,512]{1,2,0:T(8,128)}) fusion(bf16[512,4,32]{0,2,1:T(8,128)(2,1)S(1)} %bitcast.293, bf16[512,4,32]{0,2,1:T(8,128)(2,1)S(1)} %bitcast.292), kind=kOutput, calls=%fused_computation.165 | convolution fusion | flops 70255104 | bytes 4464640 | tf_op jit(solution)/shard_map/sub | solution.py:62
  43.3 0.0 copy-start.1
  43.3 2.7 %fusion.7 = bf16[4,32,512]{2,1,0:T(8,128)(2,1)S(1)} fusion(bf16[512,4,32]{0,2,1:T(8,128)(2,1)S(1)} %bitcast.291, f32[4,512,512]{1,2,0:T(8,128)} %get-tuple-element.23, f32[4,512]{1,0:T(4,128)S(1)} %get-tuple-element.22), kind=kOutput, calls=%fused_computation.10 | convolution fusion | flops 69271552 | bytes 4464640 | tf_op jit(solution)/shard_map/hqk,khd->qhd/dot_general | solution.py:64
  45.9 0.0 copy-done.1
  45.9 0.2 fusion.8
  46.9 25.8 %all_to_all.21 = bf16[64,1,8,1,128]{4,2,3,1,0:T(8,128)(2,1)S(1)} all-to-all(bf16[64,1,8,1,128]{4,2,3,1,0:T(8,128)(2,1)S(1)} %constant_dynamic-update-slice_fusion.9), channel_id=1, replica_groups=mesh['gx'=64,'gy'=8] {'gx'}, dimensions={0} | all-to-all | bytes 262144 | tf_op jit(solution)/shard_map/all_to_all | solution.py:16
  72.7 0.7 copy.12
  (80 shorter events, 1.0 us)
Async XLA Ops:
  0.0 38.5 %copy-start = (bf16[3,3,128,128]{3,2,1,0:T(8,128)(2,1)S(1)}, bf16[3,3,128,128]{3,2,1,0:T(8,128)(2,1)}, u32[]{:S(2)}) copy-start(bf16[3,3,128,128]{3,2,1,0:T(8,128)(2,1)} %param.5) | copy-start | bytes 884740
  30.4 7.7 %collective-permute-start.1 = (bf16[512,128]{1,0:T(8,128)(2,1)S(1)}, bf16[512,128]{1,0:T(8,128)(2,1)S(1)}, u32[]{:S(2)}, u32[]{:S(2)}) collective-permute-start(bf16[512,128]{1,0:T(8,128)(2,1)S(1)} %bitcast.285), channel_id=1, source_target_pairs={{8,0},{16,8},{24,16},{32,24},{40,32},{48,40},{56,48},{64,56},{72,6... | collective-permute-start | bytes 393224 | tf_op jit(solution)/shard_map/ppermute | solution.py:29
  32.7 5.2 %collective-permute-start = (bf16[512,128]{1,0:T(8,128)(2,1)S(1)}, bf16[512,128]{1,0:T(8,128)(2,1)S(1)}, u32[]{:S(2)}, u32[]{:S(2)}) collective-permute-start(bf16[512,128]{1,0:T(8,128)(2,1)S(1)} %bitcast.286), channel_id=1, source_target_pairs={{0,8},{8,16},{16,24},{24,32},{32,40},{40,48},{48,56},{56,64},{64,7... | collective-permute-start | bytes 393224 | tf_op jit(solution)/shard_map/ppermute | solution.py:28
  38.4 0.9 %copy-start.2 = (bf16[128,384]{1,0:T(8,128)(2,1)S(1)}, bf16[128,384]{1,0:T(8,128)(2,1)}, u32[]{:S(2)}) copy-start(bf16[128,384]{1,0:T(8,128)(2,1)} %param.6) | copy-start | bytes 294916
  43.3 2.7 %copy-start.1 = (bf16[128,128]{1,0:T(8,128)(2,1)S(1)}, bf16[128,128]{1,0:T(8,128)(2,1)}, u32[]{:S(2)}) copy-start(bf16[128,128]{1,0:T(8,128)(2,1)} %param.7) | copy-start | bytes 98308
